TPU v7x, 256 devices: a whole 4x4x8 slice. The times are simulated.
256 devices in a mesh: node: 8 (over z), expert: 16 (over x, y), column: 2 (over core).
Axes of the slice: x: 4, y: 4, z: 8, core: 2. Of those that a mesh axis runs over, the one named last changes fastest.
Arguments:
- slot_grads: bfloat16 [128, 768, 2048], P(('node', 'expert'), None, 'column'), may hold values from -8 to 8
- slot_tokens: int32 [128], replicated, may hold values from 16 to 511
- old_slots: int32 [128], replicated, may hold values from 0 to 79, as said below
- owner_chip: int32 [128], replicated, may hold values from 0 to 127, each once
- momentum: bfloat16 [128, 768, 2048], P(('node', 'expert'), None, 'column'), may hold values from -3 to 3
- master: float32 [128, 768, 2048], P(('node', 'expert'), None, 'column'), may hold values from -0.5 to 0.5
- new_slots: int32 [128], replicated, may hold values from 0 to 79, as said below
Outputs:
- new_momentum: bfloat16 [128, 768, 2048], P(('node', 'expert'), None, 'column')
- new_master: float32 [128, 768, 2048], P(('node', 'expert'), None, 'column')
- new_slot_weights: bfloat16 [128, 768, 2048], P(('node', 'expert'), None, 'column')
Inputs may be any that keep to these rules, and one draw needn't show every extreme that they name: `old_slots`: every expert 0 .. 79 is held by 1 to 4 slots, and some expert by exactly 4. `new_slots`: every expert 0 .. 79 is held by 1 to 4 slots, and some expert by exactly 4. Each chip position appears once; owner_chip[e] owns expert e for e below 80, and the chips named at 80 and beyond own none.
All inputs are finite; a program needn't handle non-finite values.
Results may differ from a plain program's by a relative error of at most 0.0023.
Values may be sent and summed in bfloat16 or wider, within the bound.
A program may use at most 128 MiB of HBM per device.

v0:
```python
import math

import jax
import jax.numpy as jnp
from jax import lax
from jax.experimental import pallas as pl
from jax.experimental.pallas import tpu as pltpu
from jax.sharding import PartitionSpec as P

D = 2048
FF = 768
HALF = D // 2
CHIPS = 128
EXPERTS = 80
NODES = 8
PLANE = 16
ROWS = FF // PLANE
COLS = HALF // NODES
FINE = 16
PARTS = ((FINE, ROWS - FINE), (0, FINE))
TALL = 256
WIDE = 256

coef_a = 3.4445
coef_b = -4.775
coef_c = 2.0315
momentum_beta = 0.95
learn_rate = 1.0
weight_decay = 0.1
epsilon = 1e-07
step_scale = learn_rate * 0.2 * math.sqrt(max(FF, D))

MESH = pl.DeviceIdType.MESH


def partner(step, node, spot):
    to_node = lax.rem(node + lax.rem(step, 8), 8)
    to_x = lax.rem(spot // 4 + lax.rem(step // 8, 4), 4)
    to_y = lax.rem(lax.rem(spot, 4) + step // 32, 4)
    return to_node, to_x * 4 + to_y


def part_of(ref, node, spot, part):
    first, height = PARTS[part]
    rows = pl.ds(pl.multiple_of(spot * ROWS + first, FINE), height)
    cols = pl.ds(pl.multiple_of(node * COLS, COLS), COLS)
    return ref.at[rows, cols]


def rest_of(ref, node, spot):
    rows = pl.ds(pl.multiple_of(spot * FINE, FINE), FINE)
    cols = pl.ds(pl.multiple_of(node * COLS, COLS), COLS)
    return ref.at[rows, cols]


def mul(left, right):
    return jnp.dot(left, right, preferred_element_type=jnp.float32)


def tables(tokens_ref, old_ref, owner_ref, index_ref, weight_ref):
    shape = (CHIPS, CHIPS)
    across = lax.broadcasted_iota(jnp.int32, shape, 1)
    down = lax.broadcasted_iota(jnp.int32, shape, 0)
    owner = jnp.broadcast_to(owner_ref[...], shape).T
    match = (owner == across) & (down < EXPERTS)
    owned = jnp.sum(jnp.where(match, down + 1, 0), axis=0, keepdims=True) - 1
    old = jnp.broadcast_to(old_ref[...], shape).T
    tokens = jnp.broadcast_to(tokens_ref[...], shape).T
    picked = old == owned
    total = jnp.sum(jnp.where(picked, tokens, 0), axis=0, keepdims=True)
    total = jnp.maximum(total.astype(jnp.float32), 1.0)
    for k in range(4):
        first = jnp.min(jnp.where(picked, down, CHIPS), axis=0, keepdims=True)
        here = down == first
        count = jnp.sum(jnp.where(here, tokens, 0), axis=0, keepdims=True)
        weight_ref[k : k + 1, :] = count.astype(jnp.float32) / total
        index_ref[k : k + 1, :] = jnp.where(first < CHIPS, first, 0)
        picked = picked & jnp.logical_not(here)


def step_kernel(
    grads_ref, tokens_ref, old_ref, owner_ref, momentum_ref, master_ref, new_s, owner_s,
    moment_out, master_out, slots_out,
    local, momentum, master, landing_0, landing_1, pieces_0, pieces_1, rests,
    near, rest, x_bf, part, other, gram, gram_bf, first, first_bf, both_bf, change,
    weights, arrived_0, arrived_1, chosen_0, chosen_1,
    index_v, weight_v, index_s, weight_s, copy_sems, sems,
):
    node, spot, core = (lax.axis_index(a) for a in ("node", "expert", "column"))
    me = node * PLANE + spot
    landing, pieces = (landing_0, landing_1), (pieces_0, pieces_1)
    arrived, chosen = (arrived_0, arrived_1), (chosen_0, chosen_1)

    def remote(src, dst, lane, to_node, to_spot, to_core):
        return pltpu.make_async_remote_copy(
            src, dst, sems.at[2 * lane], sems.at[2 * lane + 1],
            device_id=(to_node, to_spot, to_core), device_id_type=MESH,
        )

    def every(body):
        def wrapped(step, carry):
            body(step, *partner(step, node, spot))
            return carry

        lax.fori_loop(1, CHIPS, wrapped, 0)

    def all_of(buffer, lane):
        rows = buffer.at[pl.ds(0, CHIPS - 1)]
        return remote(rows, rows, lane, node, spot, core)

    def spread(source, targets, k, lane):
        def send(step, to_node, to_spot):
            block = part_of(source, to_node, to_spot, k)
            remote(block, targets.at[me], lane, to_node, to_spot, core).start()

        every(send)
        targets[me] = part_of(source, node, spot, k)[...]

    def deliver(make, sources, place, lane):
        def send(step):
            to_node, to_spot = partner(step, node, spot)
            src = sources.at[to_node * PLANE + to_spot]
            remote(src, place, lane, to_node, to_spot, core).start()

        def stage(step, carry):
            make(step)
            send(step - 1)
            return carry

        make(1)
        lax.fori_loop(2, CHIPS, stage, 0)
        make(0)
        send(CHIPS - 1)
        place[...] = sources[me]

    loads = (
        pltpu.make_async_copy(grads_ref.at[0], local, copy_sems.at[0]),
        pltpu.make_async_copy(momentum_ref.at[0], momentum, copy_sems.at[1]),
        pltpu.make_async_copy(master_ref.at[0], master, copy_sems.at[2]),
    )
    for load in loads:
        load.start()

    barrier = pltpu.get_barrier_semaphore()

    def greet(step, to_node, to_spot):
        pl.semaphore_signal(
            barrier, inc=1, device_id=(to_node, to_spot, core), device_id_type=MESH
        )

    every(greet)
    pl.semaphore_signal(barrier, inc=1, device_id=(node, spot, 1 - core), device_id_type=MESH)
    pl.semaphore_wait(barrier, CHIPS)
    loads[0].wait()
    for k in range(2):
        spread(local, landing[k], k, k)

    tables(tokens_ref, old_ref, owner_ref, index_v, weight_v)
    to_smem = (
        pltpu.make_async_copy(index_v, index_s, copy_sems.at[3]),
        pltpu.make_async_copy(weight_v, weight_s, copy_sems.at[4]),
    )
    for copy in to_smem:
        copy.start()
    for copy in to_smem:
        copy.wait()

    for k in range(2):
        all_of(landing[k], k).wait_recv()

        def combine(step, k=k):
            to_node, to_spot = partner(step, node, spot)
            chip = to_node * PLANE + to_spot
            total = landing[k][index_s[0, chip]].astype(jnp.float32) * weight_s[0, chip]
            for j in range(1, 4):
                slot = landing[k][index_s[j, chip]].astype(jnp.float32)
                total += slot * weight_s[j, chip]
            rounded = total.astype(jnp.bfloat16)
            pieces[k][chip] = rounded
            if k == 1:
                rests[chip] = (total - rounded.astype(jnp.float32)).astype(jnp.bfloat16)

        deliver(combine, pieces[k], part_of(near, node, spot, k), 2 + k)

    def send_rest(step, to_node, to_spot):
        src = rests.at[to_node * PLANE + to_spot]
        remote(src, rest_of(rest, node, spot), 4, to_node, to_spot, core).start()

    every(send_rest)
    rest_of(rest, node, spot)[...] = rests[me]

    def rows_of(block, k):
        start, height = PARTS[k]
        return pl.ds(pl.multiple_of(block * ROWS + start, FINE), height)

    loads[1].wait()
    for k in range(2):
        all_of(pieces[k], 2 + k).wait_recv()

        def direction(block, carry, k=k):
            rows = rows_of(block, k)
            grad = near[rows, :].astype(jnp.float32)
            moment = momentum_beta * momentum[rows, :].astype(jnp.float32) + grad
            x_bf[rows, :] = (grad + momentum_beta * moment).astype(jnp.bfloat16)
            return carry

        lax.fori_loop(0, PLANE, direction, 0)

    def band(i):
        return pl.ds(pl.multiple_of(i * TALL, TALL), TALL)

    bands = FF // TALL

    def gram_band(i, carry):
        product = lax.dot_general(
            x_bf[band(i), :], x_bf[...], (((1,), (1,)), ((), ())),
            preferred_element_type=jnp.float32,
        )
        part[band(i), :] = product.astype(jnp.bfloat16)
        return carry

    lax.fori_loop(0, bands, gram_band, 0)
    swap = remote(part, other, 5, node, spot, 1 - core)

    def own_band(i, carry):
        gram[band(i), :] = part[band(i), :].astype(jnp.float32)
        return carry

    lax.fori_loop(0, bands, own_band, 0)
    swap.start()
    swap.wait_recv()

    eye = (CHIPS, CHIPS)
    on_diagonal = lax.broadcasted_iota(jnp.int32, eye, 0) == lax.broadcasted_iota(
        jnp.int32, eye, 1
    )
    diagonal = jnp.zeros(eye, jnp.float32)
    for i in range(FF // CHIPS):
        at = slice(i * CHIPS, (i + 1) * CHIPS)
        diagonal += jnp.where(on_diagonal, gram[at, at] + other[at, at].astype(jnp.float32), 0.0)
    squares = jnp.sum(jnp.sum(diagonal, axis=0, keepdims=True), axis=1, keepdims=True)
    scale = 1.0 / (jnp.sqrt(squares) + epsilon)
    scale_2 = scale * scale

    def scale_band(i, carry):
        scaled = (gram[band(i), :] + other[band(i), :].astype(jnp.float32)) * scale_2
        gram[band(i), :] = scaled
        gram_bf[band(i), :] = scaled.astype(jnp.bfloat16)
        return carry

    lax.fori_loop(0, bands, scale_band, 0)

    def first_band(i, carry):
        value = coef_b * gram[band(i), :] + coef_c * mul(gram_bf[band(i), :], gram_bf[...])
        first[band(i), :] = value
        first_bf[band(i), :] = value.astype(jnp.bfloat16)
        return carry

    lax.fori_loop(0, bands, first_band, 0)

    def next_band(i, carry):
        half_way = coef_a * gram[band(i), :] + mul(first_bf[band(i), :], gram_bf[...])
        after = coef_a * half_way + mul(half_way.astype(jnp.bfloat16), first_bf[...])
        gram[band(i), :] = after
        return carry

    lax.fori_loop(0, bands, next_band, 0)

    def round_band(i, carry):
        gram_bf[band(i), :] = gram[band(i), :].astype(jnp.bfloat16)
        return carry

    lax.fori_loop(0, bands, round_band, 0)

    def both_band(i, carry):
        second = coef_b * gram[band(i), :] + coef_c * mul(gram_bf[band(i), :], gram_bf[...])
        value = coef_a * (first[band(i), :] + second)
        value += mul(second.astype(jnp.bfloat16), first_bf[...])
        both_bf[band(i), :] = value.astype(jnp.bfloat16)
        return carry

    lax.fori_loop(0, bands, both_band, 0)

    def change_band(i, carry):
        cols = pl.ds(pl.multiple_of(i * WIDE, WIDE), WIDE)
        change[:, cols] = mul(both_bf[...], x_bf[:, cols])
        return carry

    lax.fori_loop(0, HALF // WIDE, change_band, 0)

    loads[2].wait()
    length = step_scale * scale
    for k in range(2):
        if k == 1:
            all_of(rests, 4).wait_recv()

        def update(block, carry, k=k):
            rows = rows_of(block, k)
            grad = near[rows, :].astype(jnp.float32)
            if k == 1:
                fine_rows = pl.ds(pl.multiple_of(block * FINE, FINE), FINE)
                grad += rest[fine_rows, :].astype(jnp.float32)
            moment = momentum_beta * momentum[rows, :].astype(jnp.float32) + grad
            moment_out[rows, :] = moment.astype(jnp.bfloat16)
            iterate = (coef_a * coef_a) * (grad + momentum_beta * moment) + change[rows, :]
            value = (1.0 - learn_rate * weight_decay) * master[rows, :] - length * iterate
            master_out[rows, :] = value
            weights[rows, :] = value.astype(jnp.bfloat16)
            return carry

        lax.fori_loop(0, PLANE, update, 0)
        spread(weights, arrived[k], k, 6 + k)

    for k in range(2):
        all_of(arrived[k], 6 + k).wait_recv()

        def choose(step, k=k):
            to_node, to_spot = partner(step, node, spot)
            chip = to_node * PLANE + to_spot
            chosen[k][chip] = arrived[k][owner_s[new_s[chip]]]

        deliver(choose, chosen[k], part_of(slots_out, node, spot, k), 8 + k)

    for k in range(2):
        all_of(chosen[k], 8 + k).wait_recv()
        for lane in (0, 2, 6, 8):
            all_of(chosen[k], lane + k).wait_send()
    all_of(rests, 4).wait_send()
    swap.wait_send()


def write_kernel(moment_ref, master_ref, slots_ref, moment_out, master_out, slots_out, sems):
    copies = [
        pltpu.make_async_copy(source, target.at[0], sems.at[i])
        for i, (source, target) in enumerate(
            ((master_ref, master_out), (moment_ref, moment_out), (slots_ref, slots_out))
        )
    ]
    for copy in copies:
        copy.start()
    for copy in copies:
        copy.wait()


def on_device(slot_grads, slot_tokens, old_slots, owner_chip, momentum, master, new_slots):
    bf, f32 = jnp.bfloat16, jnp.float32
    vmem = pl.BlockSpec(memory_space=pltpu.VMEM)
    smem = pl.BlockSpec(memory_space=pltpu.SMEM)
    hbm = pl.BlockSpec(memory_space=pl.ANY)
    matrix = (FF, HALF)
    square = (FF, FF)
    tall = (CHIPS, PARTS[0][1], COLS)
    low = (CHIPS, FINE, COLS)
    row = (1, CHIPS)
    kept = (pltpu.VMEM(matrix, bf), pltpu.VMEM(matrix, f32), pltpu.VMEM(matrix, bf))
    moment_new, master_new, slots = pl.pallas_call(
        step_kernel,
        out_shape=kept,
        in_specs=[hbm, vmem, vmem, vmem, hbm, hbm, smem, smem],
        out_specs=(vmem, vmem, vmem),
        scratch_shapes=[
            pltpu.VMEM(matrix, bf),
            pltpu.VMEM(matrix, bf),
            pltpu.VMEM(matrix, f32),
            pltpu.VMEM(tall, bf),
            pltpu.VMEM(low, bf),
            pltpu.VMEM(tall, bf),
            pltpu.VMEM(low, bf),
            pltpu.VMEM(low, bf),
            pltpu.VMEM(matrix, bf),
            pltpu.VMEM((PLANE * FINE, HALF), bf),
            pltpu.VMEM(matrix, bf),
            pltpu.VMEM(square, bf),
            pltpu.VMEM(square, bf),
            pltpu.VMEM(square, f32),
            pltpu.VMEM(square, bf),
            pltpu.VMEM(square, f32),
            pltpu.VMEM(square, bf),
            pltpu.VMEM(square, bf),
            pltpu.VMEM(matrix, f32),
            pltpu.VMEM(matrix, bf),
            pltpu.VMEM(tall, bf),
            pltpu.VMEM(low, bf),
            pltpu.VMEM(tall, bf),
            pltpu.VMEM(low, bf),
            pltpu.VMEM((8, CHIPS), jnp.int32),
            pltpu.VMEM((8, CHIPS), f32),
            pltpu.SMEM((8, CHIPS), jnp.int32),
            pltpu.SMEM((8, CHIPS), f32),
            pltpu.SemaphoreType.DMA((5,)),
            pltpu.SemaphoreType.DMA((20,)),
        ],
        compiler_params=pltpu.CompilerParams(
            collective_id=0, has_side_effects=True, vmem_limit_bytes=50 * 2**20
        ),
    )(
        slot_grads,
        slot_tokens.reshape(row),
        old_slots.reshape(row),
        owner_chip.reshape(row),
        momentum,
        master,
        new_slots,
        owner_chip,
    )
    outs = tuple(jax.ShapeDtypeStruct((1, *matrix), kind) for kind in (bf, f32, bf))
    return pl.pallas_call(
        write_kernel,
        out_shape=outs,
        in_specs=[vmem, vmem, vmem],
        out_specs=(hbm, hbm, hbm),
        scratch_shapes=[pltpu.SemaphoreType.DMA((3,))],
        compiler_params=pltpu.CompilerParams(vmem_limit_bytes=2**20),
    )(moment_new, master_new, slots)


def solution(mesh):
    split = P(("node", "expert"), None, "column")
    return jax.shard_map(
        on_device,
        mesh=mesh,
        in_specs=(split, P(), P(), P(), split, split, P()),
        out_specs=(split, split, split),
        check_vma=False,
    )
```

profile of v0, /device:TPU:1, one launch (start us, length us, event | category | flops | bytes accessed | tf_op | source)
XLA Modules:
  0.0 179.4 jit_solution(572859761896589360)
XLA Ops:
  0.6 176.0 %shard_map.94 = (bf16[768,1024]{1,0:T(8,128)(2,1)S(1)}, f32[768,1024]{1,0:T(8,128)S(1)}, bf16[768,1024]{1,0:T(8,128)(2,1)S(1)}) custom-call(bf16[1,768,1024]{2,1,0:T(8,128)(2,1)} %grads_ref.1, s32[1,128]{1,0:T(1,128)} %bitcast.4, s32[1,128]{1,0:T(1,128)} %bitcast.5, s32[1,128]{1,0:T(1,128)} %bitcast.3, bf16[1,768,1024]{2,1,0:T(8,128)(2,1)} %momentum_ref.1, ...), custom_call_target="tpu_custom_call" | custom-call | tf_op jit(solution)/shard_map/pallas_call | solution.py:356
  176.7 2.7 %shard_map.95 = (bf16[1,768,1024]{2,1,0:T(8,128)(2,1)}, f32[1,768,1024]{2,1,0:T(8,128)}, bf16[1,768,1024]{2,1,0:T(8,128)(2,1)}) custom-call(bf16[768,1024]{1,0:T(8,128)(2,1)S(1)} %get-tuple-element.6.moment_ref, f32[768,1024]{1,0:T(8,128)S(1)} %get-tuple-element.7.master_ref, bf16[768,1024]{1,0:T(8,128)(2,1)S(1)} %get-tuple-element.8.slots_ref), custom_call_target="tpu_custom_call" | custom-call | tf_op jit(solution)/shard_map/pallas_call | solution.py:407
where the time goes:
time: 179 us
  Pallas kernels  179 us (100%)
    pallas_call x1, Pallas kernels, on_device(): pl.pallas_call(step_kernel, out_shape=kept, in_specs=[hbm, vmem, vmem, vm...  176 us

commit v1 on v0

--- a/solution.py
+++ b/solution.py
@@ -18,7 +18,6 @@
 COLS = HALF // NODES
 FINE = 16
 PARTS = ((FINE, ROWS - FINE), (0, FINE))
-TALL = 256
 WIDE = 256
 
 coef_a = 3.4445
@@ -28,6 +27,7 @@
 learn_rate = 1.0
 weight_decay = 0.1
 epsilon = 1e-07
+code_scale = 2.0**27
 step_scale = learn_rate * 0.2 * math.sqrt(max(FF, D))
 
 MESH = pl.DeviceIdType.MESH
@@ -47,10 +47,16 @@
     return ref.at[rows, cols]
 
 
-def rest_of(ref, node, spot):
-    rows = pl.ds(pl.multiple_of(spot * FINE, FINE), FINE)
-    cols = pl.ds(pl.multiple_of(node * COLS, COLS), COLS)
-    return ref.at[rows, cols]
+def coded(grad):
+    large = grad * code_scale
+    return ((large * large) * (large * jnp.abs(large))).astype(jnp.bfloat16)
+
+
+def decoded(code):
+    code = code.astype(jnp.float32)
+    size = lax.rsqrt(lax.rsqrt(jnp.abs(code))) * (1.0 / code_scale)
+    size = jnp.where(code == 0.0, 0.0, size)
+    return jnp.where(code < 0.0, -size, size)
 
 
 def mul(left, right):
@@ -81,8 +87,8 @@
 def step_kernel(
     grads_ref, tokens_ref, old_ref, owner_ref, momentum_ref, master_ref, new_s, owner_s,
     moment_out, master_out, slots_out,
-    local, momentum, master, landing_0, landing_1, pieces_0, pieces_1, rests,
-    near, rest, x_bf, part, other, gram, gram_bf, first, first_bf, both_bf, change,
+    local, momentum, master, landing_0, landing_1, pieces_0, pieces_1,
+    near, nesterov, x_bf, part, other, gram, gram_bf, first, first_bf, next_bf, both_bf, change,
     weights, arrived_0, arrived_1, chosen_0, chosen_1,
     index_v, weight_v, index_s, weight_s, copy_sems, sems,
 ):
@@ -97,19 +103,30 @@
             device_id=(to_node, to_spot, to_core), device_id_type=MESH,
         )
 
+    near_nodes = [lax.rem(node + by_node, NODES) for by_node in range(NODES)]
+
+    def spot_at(step):
+        to_x = lax.rem(spot // 4 + step // 4, 4)
+        return to_x * 4 + lax.rem(lax.rem(spot, 4) + lax.rem(step, 4), 4)
+
     def every(body):
+        for to_node in near_nodes[1:]:
+            body(to_node, spot)
+
         def wrapped(step, carry):
-            body(step, *partner(step, node, spot))
-            return carry
-
-        lax.fori_loop(1, CHIPS, wrapped, 0)
+            to_spot = spot_at(step)
+            for to_node in near_nodes:
+                body(to_node, to_spot)
+            return carry
+
+        lax.fori_loop(1, PLANE, wrapped, 0)
 
     def all_of(buffer, lane):
         rows = buffer.at[pl.ds(0, CHIPS - 1)]
         return remote(rows, rows, lane, node, spot, core)
 
     def spread(source, targets, k, lane):
-        def send(step, to_node, to_spot):
+        def send(to_node, to_spot):
             block = part_of(source, to_node, to_spot, k)
             remote(block, targets.at[me], lane, to_node, to_spot, core).start()
 
@@ -143,7 +160,7 @@
 
     barrier = pltpu.get_barrier_semaphore()
 
-    def greet(step, to_node, to_spot):
+    def greet(to_node, to_spot):
         pl.semaphore_signal(
             barrier, inc=1, device_id=(to_node, to_spot, core), device_id_type=MESH
         )
@@ -165,29 +182,58 @@
     for copy in to_smem:
         copy.wait()
 
-    for k in range(2):
-        all_of(landing[k], k).wait_recv()
-
-        def combine(step, k=k):
-            to_node, to_spot = partner(step, node, spot)
-            chip = to_node * PLANE + to_spot
-            total = landing[k][index_s[0, chip]].astype(jnp.float32) * weight_s[0, chip]
-            for j in range(1, 4):
-                slot = landing[k][index_s[j, chip]].astype(jnp.float32)
-                total += slot * weight_s[j, chip]
-            rounded = total.astype(jnp.bfloat16)
-            pieces[k][chip] = rounded
-            if k == 1:
-                rests[chip] = (total - rounded.astype(jnp.float32)).astype(jnp.bfloat16)
-
-        deliver(combine, pieces[k], part_of(near, node, spot, k), 2 + k)
-
-    def send_rest(step, to_node, to_spot):
-        src = rests.at[to_node * PLANE + to_spot]
-        remote(src, rest_of(rest, node, spot), 4, to_node, to_spot, core).start()
-
-    every(send_rest)
-    rest_of(rest, node, spot)[...] = rests[me]
+    parity = lax.rem(node + spot // 4 + lax.rem(spot, 4), 2)
+
+    def combine(chip, k):
+        total = landing[k][index_s[0, chip]].astype(jnp.float32) * weight_s[0, chip]
+        for j in range(1, 4):
+            slot = landing[k][index_s[j, chip]].astype(jnp.float32)
+            total += slot * weight_s[j, chip]
+        pieces[k][chip] = coded(total)
+
+    def combine_half(half, k):
+        offset = lax.rem(parity + half, 2)
+        place = part_of(near, node, spot, k)
+
+        def chips_at(step):
+            odd = lax.rem(offset + step // 4 + lax.rem(step, 4), 2)
+            nodes = [lax.rem(node + odd + by_node, NODES) for by_node in range(0, NODES, 2)]
+            return nodes, spot_at(step)
+
+        def make(step):
+            nodes, to_spot = chips_at(step)
+            for to_node in nodes:
+                combine(to_node * PLANE + to_spot, k)
+
+        def send(step, skip_own=False):
+            nodes, to_spot = chips_at(step)
+            for i, to_node in enumerate(nodes):
+                src = pieces[k].at[to_node * PLANE + to_spot]
+                copy = remote(src, place, 2 + k, to_node, to_spot, core)
+                if skip_own and i == 0:
+                    pl.when(offset == 1)(copy.start)
+                else:
+                    copy.start()
+
+        def stage(step, carry):
+            make(step)
+            send(step - 1)
+            return carry
+
+        make(0)
+        make(1)
+        send(0, skip_own=True)
+        lax.fori_loop(2, PLANE, stage, 0)
+        if half == 1:
+            combine(me, k)
+            place[...] = pieces[k][me]
+        send(PLANE - 1)
+
+    for half in range(2):
+        for k in range(2):
+            if half == 0:
+                all_of(landing[k], k).wait_recv()
+            combine_half(half, k)
 
     def rows_of(block, k):
         start, height = PARTS[k]
@@ -199,117 +245,102 @@
 
         def direction(block, carry, k=k):
             rows = rows_of(block, k)
-            grad = near[rows, :].astype(jnp.float32)
+            grad = decoded(near[rows, :])
             moment = momentum_beta * momentum[rows, :].astype(jnp.float32) + grad
-            x_bf[rows, :] = (grad + momentum_beta * moment).astype(jnp.bfloat16)
-            return carry
-
-        lax.fori_loop(0, PLANE, direction, 0)
-
-    def band(i):
-        return pl.ds(pl.multiple_of(i * TALL, TALL), TALL)
-
-    bands = FF // TALL
-
-    def gram_band(i, carry):
+            moment_out[rows, :] = moment.astype(jnp.bfloat16)
+            ahead = grad + momentum_beta * moment
+            nesterov[rows, :] = ahead
+            x_bf[rows, :] = ahead.astype(jnp.bfloat16)
+            return carry
+
+        lax.fori_loop(0, PLANE, direction, 0, unroll=2)
+
+    bands = [pl.ds(i * WIDE, WIDE) for i in range(FF // WIDE)]
+
+    def swap_band(i):
+        at = (slice(None), bands[i])
+        return remote(part.at[at], other.at[at], 5, node, spot, 1 - core)
+
+    for i, cols in enumerate(bands):
         product = lax.dot_general(
-            x_bf[band(i), :], x_bf[...], (((1,), (1,)), ((), ())),
+            x_bf[...], x_bf[cols, :], (((1,), (1,)), ((), ())),
             preferred_element_type=jnp.float32,
         )
-        part[band(i), :] = product.astype(jnp.bfloat16)
-        return carry
-
-    lax.fori_loop(0, bands, gram_band, 0)
-    swap = remote(part, other, 5, node, spot, 1 - core)
-
-    def own_band(i, carry):
-        gram[band(i), :] = part[band(i), :].astype(jnp.float32)
-        return carry
-
-    lax.fori_loop(0, bands, own_band, 0)
-    swap.start()
-    swap.wait_recv()
-
+        part[:, cols] = product.astype(jnp.bfloat16)
+        if i > 0:
+            swap_band(i - 1).start()
     eye = (CHIPS, CHIPS)
     on_diagonal = lax.broadcasted_iota(jnp.int32, eye, 0) == lax.broadcasted_iota(
         jnp.int32, eye, 1
     )
-    diagonal = jnp.zeros(eye, jnp.float32)
-    for i in range(FF // CHIPS):
-        at = slice(i * CHIPS, (i + 1) * CHIPS)
-        diagonal += jnp.where(on_diagonal, gram[at, at] + other[at, at].astype(jnp.float32), 0.0)
+
+    def diagonal_of(ref):
+        total = jnp.zeros(eye, jnp.float32)
+        for i in range(FF // CHIPS):
+            at = slice(i * CHIPS, (i + 1) * CHIPS)
+            total += jnp.where(on_diagonal, ref[at, at].astype(jnp.float32), 0.0)
+        return total
+
+    diagonal = diagonal_of(part)
+    swap_band(len(bands) - 1).start()
+    remote(part, other, 5, node, spot, 1 - core).wait_recv()
+    diagonal += diagonal_of(other)
     squares = jnp.sum(jnp.sum(diagonal, axis=0, keepdims=True), axis=1, keepdims=True)
     scale = 1.0 / (jnp.sqrt(squares) + epsilon)
     scale_2 = scale * scale
-
-    def scale_band(i, carry):
-        scaled = (gram[band(i), :] + other[band(i), :].astype(jnp.float32)) * scale_2
-        gram[band(i), :] = scaled
-        gram_bf[band(i), :] = scaled.astype(jnp.bfloat16)
-        return carry
-
-    lax.fori_loop(0, bands, scale_band, 0)
-
-    def first_band(i, carry):
-        value = coef_b * gram[band(i), :] + coef_c * mul(gram_bf[band(i), :], gram_bf[...])
-        first[band(i), :] = value
-        first_bf[band(i), :] = value.astype(jnp.bfloat16)
-        return carry
-
-    lax.fori_loop(0, bands, first_band, 0)
-
-    def next_band(i, carry):
-        half_way = coef_a * gram[band(i), :] + mul(first_bf[band(i), :], gram_bf[...])
-        after = coef_a * half_way + mul(half_way.astype(jnp.bfloat16), first_bf[...])
-        gram[band(i), :] = after
-        return carry
-
-    lax.fori_loop(0, bands, next_band, 0)
-
-    def round_band(i, carry):
-        gram_bf[band(i), :] = gram[band(i), :].astype(jnp.bfloat16)
-        return carry
-
-    lax.fori_loop(0, bands, round_band, 0)
-
-    def both_band(i, carry):
-        second = coef_b * gram[band(i), :] + coef_c * mul(gram_bf[band(i), :], gram_bf[...])
-        value = coef_a * (first[band(i), :] + second)
-        value += mul(second.astype(jnp.bfloat16), first_bf[...])
-        both_bf[band(i), :] = value.astype(jnp.bfloat16)
-        return carry
-
-    lax.fori_loop(0, bands, both_band, 0)
-
-    def change_band(i, carry):
-        cols = pl.ds(pl.multiple_of(i * WIDE, WIDE), WIDE)
-        change[:, cols] = mul(both_bf[...], x_bf[:, cols])
-        return carry
-
-    lax.fori_loop(0, HALF // WIDE, change_band, 0)
+    for cols in bands:
+        both = part[:, cols].astype(jnp.float32) + other[:, cols].astype(jnp.float32)
+        scaled = both * scale_2
+        gram[:, cols] = scaled
+        gram_bf[:, cols] = scaled.astype(jnp.bfloat16)
+
+    for cols in bands:
+        value = coef_b * gram[:, cols] + coef_c * mul(gram_bf[...], gram_bf[:, cols])
+        first[:, cols] = value
+        first_bf[:, cols] = value.astype(jnp.bfloat16)
+    for cols in bands:
+        half_way = coef_a * gram[:, cols] + mul(first_bf[...], gram_bf[:, cols])
+        after = coef_a * half_way + mul(first_bf[...], half_way.astype(jnp.bfloat16))
+        gram[:, cols] = after
+        next_bf[:, cols] = after.astype(jnp.bfloat16)
+    for cols in bands:
+        second = coef_b * gram[:, cols] + coef_c * mul(next_bf[...], next_bf[:, cols])
+        value = coef_a * (first[:, cols] + second)
+        value += mul(first_bf[...], second.astype(jnp.bfloat16))
+        both_bf[:, cols] = value.astype(jnp.bfloat16)
 
     loads[2].wait()
     length = step_scale * scale
-    for k in range(2):
-        if k == 1:
-            all_of(rests, 4).wait_recv()
-
-        def update(block, carry, k=k):
-            rows = rows_of(block, k)
-            grad = near[rows, :].astype(jnp.float32)
-            if k == 1:
-                fine_rows = pl.ds(pl.multiple_of(block * FINE, FINE), FINE)
-                grad += rest[fine_rows, :].astype(jnp.float32)
-            moment = momentum_beta * momentum[rows, :].astype(jnp.float32) + grad
-            moment_out[rows, :] = moment.astype(jnp.bfloat16)
-            iterate = (coef_a * coef_a) * (grad + momentum_beta * moment) + change[rows, :]
-            value = (1.0 - learn_rate * weight_decay) * master[rows, :] - length * iterate
-            master_out[rows, :] = value
-            weights[rows, :] = value.astype(jnp.bfloat16)
-            return carry
-
-        lax.fori_loop(0, PLANE, update, 0)
-        spread(weights, arrived[k], k, 6 + k)
+
+    pairs = NODES // 2
+    for i in range(pairs):
+        pair = lax.rem(node // 2 + i, pairs)
+        cols = pl.ds(pl.multiple_of(pair * WIDE, WIDE), WIDE)
+        change[:, cols] = mul(both_bf[...], x_bf[:, cols])
+
+        def update(block, carry, cols=cols):
+            rows = pl.ds(pl.multiple_of(block * ROWS, ROWS), ROWS)
+            iterate = (coef_a * coef_a) * nesterov[rows, cols] + change[rows, cols]
+            value = (1.0 - learn_rate * weight_decay) * master[rows, cols] - length * iterate
+            master_out[rows, cols] = value
+            weights[rows, cols] = value.astype(jnp.bfloat16)
+            return carry
+
+        lax.fori_loop(0, PLANE, update, 0, unroll=4)
+
+        def send_weights(step, carry, pair=pair):
+            to_node = 2 * pair + lax.rem(node + step, 2)
+            to_x = lax.rem(spot // 4 + lax.rem(step // 2, 4), 4)
+            to_y = lax.rem(lax.rem(spot, 4) + step // 8, 4)
+            to_spot = to_x * 4 + to_y
+            block = part_of(weights, to_node, to_spot, 0)
+            remote(block, arrived[0].at[me], 6, to_node, to_spot, core).start()
+            return carry
+
+        lax.fori_loop(1 if i == 0 else 0, 2 * PLANE, send_weights, 0)
+
+    spread(weights, arrived[1], 1, 7)
+    arrived[0][me] = part_of(weights, node, spot, 0)[...]
 
     for k in range(2):
         all_of(arrived[k], 6 + k).wait_recv()
@@ -325,8 +356,7 @@
         all_of(chosen[k], 8 + k).wait_recv()
         for lane in (0, 2, 6, 8):
             all_of(chosen[k], lane + k).wait_send()
-    all_of(rests, 4).wait_send()
-    swap.wait_send()
+    remote(part, other, 5, node, spot, 1 - core).wait_send()
 
 
 def write_kernel(moment_ref, master_ref, slots_ref, moment_out, master_out, slots_out, sems):
@@ -366,15 +396,15 @@
             pltpu.VMEM(low, bf),
             pltpu.VMEM(tall, bf),
             pltpu.VMEM(low, bf),
-            pltpu.VMEM(low, bf),
             pltpu.VMEM(matrix, bf),
-            pltpu.VMEM((PLANE * FINE, HALF), bf),
+            pltpu.VMEM(matrix, f32),
             pltpu.VMEM(matrix, bf),
             pltpu.VMEM(square, bf),
             pltpu.VMEM(square, bf),
             pltpu.VMEM(square, f32),
             pltpu.VMEM(square, bf),
             pltpu.VMEM(square, f32),
+            pltpu.VMEM(square, bf),
             pltpu.VMEM(square, bf),
             pltpu.VMEM(square, bf),
             pltpu.VMEM(matrix, f32),

time: 179 us -> 166 us (0.927)
  Pallas kernels: 179 us -> 166 us
    pallas_call x1, Pallas kernels: 176 us -> 163 us  [on_device(): pl.pallas_call(step_kernel, out_shape=kept, in_specs=[hbm, vmem, vmem, vm...]
where the time goes in v1:
time: 166 us
  Pallas kernels  166 us (100%)
    pallas_call x1, Pallas kernels, on_device(): pl.pallas_call(step_kernel, out_shape=kept, in_specs=[hbm, vmem, vmem, vm...  163 us

profile of v1, /device:TPU:1, one launch (start us, length us, event | category | flops | bytes accessed | tf_op | source)
XLA Modules:
  0.0 166.3 jit_solution(16197743130349444740)
XLA Ops:
  0.6 162.9 %shard_map.94 = (bf16[768,1024]{1,0:T(8,128)(2,1)S(1)}, f32[768,1024]{1,0:T(8,128)S(1)}, bf16[768,1024]{1,0:T(8,128)(2,1)S(1)}) custom-call(bf16[1,768,1024]{2,1,0:T(8,128)(2,1)} %grads_ref.1, s32[1,128]{1,0:T(1,128)} %bitcast.4, s32[1,128]{1,0:T(1,128)} %bitcast.5, s32[1,128]{1,0:T(1,128)} %bitcast.3, bf16[1,768,1024]{2,1,0:T(8,128)(2,1)} %momentum_ref.1, ...), custom_call_target="tpu_custom_call" | custom-call | tf_op jit(solution)/shard_map/pallas_call | solution.py:386
  163.5 2.7 %shard_map.95 = (bf16[1,768,1024]{2,1,0:T(8,128)(2,1)}, f32[1,768,1024]{2,1,0:T(8,128)}, bf16[1,768,1024]{2,1,0:T(8,128)(2,1)}) custom-call(bf16[768,1024]{1,0:T(8,128)(2,1)S(1)} %get-tuple-element.6.moment_ref, f32[768,1024]{1,0:T(8,128)S(1)} %get-tuple-element.7.master_ref, bf16[768,1024]{1,0:T(8,128)(2,1)S(1)} %get-tuple-element.8.slots_ref), custom_call_target="tpu_custom_call" | custom-call | tf_op jit(solution)/shard_map/pallas_call | solution.py:437

commit v2 on v1

--- a/solution.py
+++ b/solution.py
@@ -19,6 +19,7 @@
 FINE = 16
 PARTS = ((FINE, ROWS - FINE), (0, FINE))
 WIDE = 256
+EARLY = PLANE * PARTS[0][1]
 
 coef_a = 3.4445
 coef_b = -4.775
@@ -239,6 +240,22 @@
         start, height = PARTS[k]
         return pl.ds(pl.multiple_of(block * ROWS + start, FINE), height)
 
+    def packed(block, k):
+        height = PARTS[k][1]
+        return pl.ds(pl.multiple_of(k * EARLY + block * height, FINE), height)
+
+    def gram_part(rows, cols):
+        product = lax.dot_general(
+            x_bf[rows, :], x_bf[cols, :], (((1,), (1,)), ((), ())),
+            preferred_element_type=jnp.float32,
+        )
+        part[rows, cols] = product.astype(jnp.bfloat16)
+
+    def swap_part(rows, cols):
+        at = (rows, cols)
+        remote(part.at[at], other.at[at], 5, node, spot, 1 - core).start()
+
+    early, late, full = pl.ds(0, EARLY), pl.ds(EARLY, FF - EARLY), pl.ds(0, FF)
     loads[1].wait()
     for k in range(2):
         all_of(pieces[k], 2 + k).wait_recv()
@@ -250,25 +267,21 @@
             moment_out[rows, :] = moment.astype(jnp.bfloat16)
             ahead = grad + momentum_beta * moment
             nesterov[rows, :] = ahead
-            x_bf[rows, :] = ahead.astype(jnp.bfloat16)
-            return carry
-
-        lax.fori_loop(0, PLANE, direction, 0, unroll=2)
+            x_bf[packed(block, k), :] = ahead.astype(jnp.bfloat16)
+            return carry
+
+        lax.fori_loop(0, PLANE, direction, 0, unroll=4)
+        if k == 0:
+            for i in range(EARLY // WIDE):
+                gram_part(early, pl.ds(i * WIDE, WIDE))
+            for i in range(EARLY // WIDE):
+                swap_part(early, pl.ds(i * WIDE, WIDE))
 
     bands = [pl.ds(i * WIDE, WIDE) for i in range(FF // WIDE)]
 
-    def swap_band(i):
-        at = (slice(None), bands[i])
-        return remote(part.at[at], other.at[at], 5, node, spot, 1 - core)
-
-    for i, cols in enumerate(bands):
-        product = lax.dot_general(
-            x_bf[...], x_bf[cols, :], (((1,), (1,)), ((), ())),
-            preferred_element_type=jnp.float32,
-        )
-        part[:, cols] = product.astype(jnp.bfloat16)
-        if i > 0:
-            swap_band(i - 1).start()
+    gram_part(full, late)
+    gram_part(late, early)
+    swap_part(full, late)
     eye = (CHIPS, CHIPS)
     on_diagonal = lax.broadcasted_iota(jnp.int32, eye, 0) == lax.broadcasted_iota(
         jnp.int32, eye, 1
@@ -282,7 +295,7 @@
         return total
 
     diagonal = diagonal_of(part)
-    swap_band(len(bands) - 1).start()
+    swap_part(late, early)
     remote(part, other, 5, node, spot, 1 - core).wait_recv()
     diagonal += diagonal_of(other)
     squares = jnp.sum(jnp.sum(diagonal, axis=0, keepdims=True), axis=1, keepdims=True)
@@ -313,17 +326,20 @@
     length = step_scale * scale
 
     pairs = NODES // 2
-    for i in range(pairs):
+    for i in (2, 1, 3, 0):
         pair = lax.rem(node // 2 + i, pairs)
         cols = pl.ds(pl.multiple_of(pair * WIDE, WIDE), WIDE)
         change[:, cols] = mul(both_bf[...], x_bf[:, cols])
 
         def update(block, carry, cols=cols):
-            rows = pl.ds(pl.multiple_of(block * ROWS, ROWS), ROWS)
-            iterate = (coef_a * coef_a) * nesterov[rows, cols] + change[rows, cols]
-            value = (1.0 - learn_rate * weight_decay) * master[rows, cols] - length * iterate
-            master_out[rows, cols] = value
-            weights[rows, cols] = value.astype(jnp.bfloat16)
+            for k in range(2):
+                rows = rows_of(block, k)
+                iterate = (coef_a * coef_a) * nesterov[rows, cols]
+                iterate += change[packed(block, k), cols]
+                kept = (1.0 - learn_rate * weight_decay) * master[rows, cols]
+                value = kept - length * iterate
+                master_out[rows, cols] = value
+                weights[rows, cols] = value.astype(jnp.bfloat16)
             return carry
 
         lax.fori_loop(0, PLANE, update, 0, unroll=4)
@@ -360,12 +376,14 @@
 
 
 def write_kernel(moment_ref, master_ref, slots_ref, moment_out, master_out, slots_out, sems):
-    copies = [
-        pltpu.make_async_copy(source, target.at[0], sems.at[i])
-        for i, (source, target) in enumerate(
-            ((master_ref, master_out), (moment_ref, moment_out), (slots_ref, slots_out))
-        )
-    ]
+    copies = []
+    for source, target in (
+        (master_ref, master_out), (moment_ref, moment_out), (slots_ref, slots_out)
+    ):
+        for i in range(FF // WIDE):
+            rows = pl.ds(i * WIDE, WIDE)
+            sem = sems.at[len(copies)]
+            copies.append(pltpu.make_async_copy(source.at[rows], target.at[0, rows], sem))
     for copy in copies:
         copy.start()
     for copy in copies:
@@ -439,7 +457,7 @@
         out_shape=outs,
         in_specs=[vmem, vmem, vmem],
         out_specs=(hbm, hbm, hbm),
-        scratch_shapes=[pltpu.SemaphoreType.DMA((3,))],
+        scratch_shapes=[pltpu.SemaphoreType.DMA((9,))],
         compiler_params=pltpu.CompilerParams(vmem_limit_bytes=2**20),
     )(moment_new, master_new, slots)
 

time: 166 us -> 165 us (level)
  Pallas kernels: 166 us -> 164 us
where the time goes in v2:
time: 165 us
  Pallas kernels  164 us (99%)
    pallas_call x1, Pallas kernels, on_device(): pl.pallas_call(step_kernel, out_shape=kept, in_specs=[hbm, vmem, vmem, vm...  161 us

profile of v2, /device:TPU:1, one launch (start us, length us, event | category | flops | bytes accessed | tf_op | source)
XLA Modules:
  0.0 164.6 jit_solution(7276314056138969603)
XLA Ops:
  0.6 161.3 %shard_map.94 = (bf16[768,1024]{1,0:T(8,128)(2,1)S(1)}, f32[768,1024]{1,0:T(8,128)S(1)}, bf16[768,1024]{1,0:T(8,128)(2,1)S(1)}) custom-call(bf16[1,768,1024]{2,1,0:T(8,128)(2,1)} %grads_ref.1, s32[1,128]{1,0:T(1,128)} %bitcast.4, s32[1,128]{1,0:T(1,128)} %bitcast.5, s32[1,128]{1,0:T(1,128)} %bitcast.3, bf16[1,768,1024]{2,1,0:T(8,128)(2,1)} %momentum_ref.1, ...), custom_call_target="tpu_custom_call" | custom-call | tf_op jit(solution)/shard_map/pallas_call | solution.py:404
  161.9 2.7 %shard_map.95 = (bf16[1,768,1024]{2,1,0:T(8,128)(2,1)}, f32[1,768,1024]{2,1,0:T(8,128)}, bf16[1,768,1024]{2,1,0:T(8,128)(2,1)}) custom-call(bf16[768,1024]{1,0:T(8,128)(2,1)S(1)} %get-tuple-element.6.moment_ref, f32[768,1024]{1,0:T(8,128)S(1)} %get-tuple-element.7.master_ref, bf16[768,1024]{1,0:T(8,128)(2,1)S(1)} %get-tuple-element.8.slots_ref), custom_call_target="tpu_custom_call" | custom-call | tf_op jit(solution)/shard_map/pallas_call | solution.py:455

commit v3 on v2

--- a/solution.py
+++ b/solution.py
@@ -32,13 +32,6 @@
 step_scale = learn_rate * 0.2 * math.sqrt(max(FF, D))
 
 MESH = pl.DeviceIdType.MESH
-
-
-def partner(step, node, spot):
-    to_node = lax.rem(node + lax.rem(step, 8), 8)
-    to_x = lax.rem(spot // 4 + lax.rem(step // 8, 4), 4)
-    to_y = lax.rem(lax.rem(spot, 4) + step // 32, 4)
-    return to_node, to_x * 4 + to_y
 
 
 def part_of(ref, node, spot, part):
@@ -135,21 +128,28 @@
         targets[me] = part_of(source, node, spot, k)[...]
 
     def deliver(make, sources, place, lane):
-        def send(step):
-            to_node, to_spot = partner(step, node, spot)
-            src = sources.at[to_node * PLANE + to_spot]
-            remote(src, place, lane, to_node, to_spot, core).start()
+        def make_step(step):
+            to_spot = spot_at(step)
+            for to_node in near_nodes:
+                make(to_node * PLANE + to_spot)
+
+        def send_step(step, nodes=near_nodes):
+            to_spot = spot_at(step)
+            for to_node in nodes:
+                src = sources.at[to_node * PLANE + to_spot]
+                remote(src, place, lane, to_node, to_spot, core).start()
 
         def stage(step, carry):
-            make(step)
-            send(step - 1)
-            return carry
-
-        make(1)
-        lax.fori_loop(2, CHIPS, stage, 0)
-        make(0)
-        send(CHIPS - 1)
+            make_step(step)
+            send_step(step - 1)
+            return carry
+
+        make_step(0)
+        make_step(1)
+        send_step(0, near_nodes[1:])
+        lax.fori_loop(2, PLANE, stage, 0)
         place[...] = sources[me]
+        send_step(PLANE - 1)
 
     loads = (
         pltpu.make_async_copy(grads_ref.at[0], local, copy_sems.at[0]),
@@ -361,9 +361,7 @@
     for k in range(2):
         all_of(arrived[k], 6 + k).wait_recv()
 
-        def choose(step, k=k):
-            to_node, to_spot = partner(step, node, spot)
-            chip = to_node * PLANE + to_spot
+        def choose(chip, k=k):
             chosen[k][chip] = arrived[k][owner_s[new_s[chip]]]
 
         deliver(choose, chosen[k], part_of(slots_out, node, spot, k), 8 + k)

time: 165 us -> 165 us (level)
  no operation moved by 1% of the time
where the time goes in v3:
time: 165 us
  Pallas kernels  165 us (100%)
    pallas_call x1, Pallas kernels, on_device(): pl.pallas_call(step_kernel, out_shape=kept, in_specs=[hbm, vmem, vmem, vm...  162 us

profile of v3, /device:TPU:1, one launch (start us, length us, event | category | flops | bytes accessed | tf_op | source)
XLA Modules:
  0.0 165.4 jit_solution(1245803292998774027)
XLA Ops:
  0.6 162.0 %shard_map.94 = (bf16[768,1024]{1,0:T(8,128)(2,1)S(1)}, f32[768,1024]{1,0:T(8,128)S(1)}, bf16[768,1024]{1,0:T(8,128)(2,1)S(1)}) custom-call(bf16[1,768,1024]{2,1,0:T(8,128)(2,1)} %grads_ref.1, s32[1,128]{1,0:T(1,128)} %bitcast.4, s32[1,128]{1,0:T(1,128)} %bitcast.5, s32[1,128]{1,0:T(1,128)} %bitcast.3, bf16[1,768,1024]{2,1,0:T(8,128)(2,1)} %momentum_ref.1, ...), custom_call_target="tpu_custom_call" | custom-call | tf_op jit(solution)/shard_map/pallas_call | solution.py:402
  162.6 2.7 %shard_map.95 = (bf16[1,768,1024]{2,1,0:T(8,128)(2,1)}, f32[1,768,1024]{2,1,0:T(8,128)}, bf16[1,768,1024]{2,1,0:T(8,128)(2,1)}) custom-call(bf16[768,1024]{1,0:T(8,128)(2,1)S(1)} %get-tuple-element.6.moment_ref, f32[768,1024]{1,0:T(8,128)S(1)} %get-tuple-element.7.master_ref, bf16[768,1024]{1,0:T(8,128)(2,1)S(1)} %get-tuple-element.8.slots_ref), custom_call_target="tpu_custom_call" | custom-call | tf_op jit(solution)/shard_map/pallas_call | solution.py:453
